TPU v7x, 256 devices: a whole 4x4x8 slice. The times are simulated.
256 devices in a mesh: expert: 16 (over x, y), dp: 16 (over z, core).
Axes of the slice: x: 4, y: 4, z: 8, core: 2. Of those that a mesh axis runs over, the one named last changes fastest.
Arguments:
- tokens: bfloat16 [2, 32768, 1280], P(None, ('expert', 'dp')), may hold values from -6 to 6
- modality: int32 [2, 32768], P(None, ('expert', 'dp')), may hold values from 0 to 1, as said below
- routes: int32 [2, 32768, 1], P(None, ('expert', 'dp')), may hold values from 0 to 15; in each aligned block of 128 rows (0 to 127, 128 to 255, ..., all dimensions but the last counted through in order) at most 16 rows name the same one
- router: bfloat16 [1280, 16], replicated, may hold values from -0.15625 to 0.15625
- w_in: bfloat16 [16, 1280, 5120], P('expert', 'dp'), may hold values from -0.15625 to 0.15625
- w_out: bfloat16 [16, 5120, 1280], P('expert', 'dp'), may hold values from -0.078125 to 0.078125
Outputs:
- mixed: bfloat16 [2, 32768, 1280], P(None, ('expert', 'dp'))
- load: float32 [2, 2, 16], replicated
Inputs may be any that keep to these rules, and one draw needn't show every extreme that they name: `routes`: among the 128 tokens of one micro-batch on one device (aligned blocks of 128 rows), at most 16 are routed to any one expert. `modality`: in every aligned block of 128 tokens of a micro-batch, the number of text tokens lies between 32 and 96.
All inputs are finite; a program needn't handle non-finite values.
Results may differ from a plain program's by a relative error of at most 0.0057.
Values may be sent and summed in bfloat16 or wider, within the bound.
No kernel may reach another device: no remote copies, remote signals or barrier semaphores. Data moves between devices by JAX's collectives and lax.ppermute only.
A program may use at most 192 MiB of HBM per device.

v0:
```python
import jax
import jax.numpy as jnp
from jax import lax
from jax.sharding import Mesh
from jax.sharding import PartitionSpec as P

EXPERT = ("expert_0", "expert_1")
DP = ("dp_0", "dp_1")
EXPERT_DP = ("expert_0", "expert_1", "dp_0", "dp_1")


def over_axes(shard, axes):
    for axis in axes:
        shard = lax.psum(shard, axis)
    return shard


def on_device(tokens, modality, routes, router, w_in, w_out):
    micro_count, tok_count, model_width = tokens.shape
    experts = router.shape[1]
    capacity = 2 * tok_count // experts
    logits = jnp.einsum("mtd,de->mte", tokens, router, preferred_element_type=jnp.float32)
    onehot = (routes == jnp.arange(experts, dtype=jnp.int32)[None, None, :]).astype(jnp.float32)
    gating = jax.nn.sigmoid(jnp.sum(logits * onehot, axis=-1))
    running = jnp.cumsum(onehot, axis=1)
    slot_pos = jnp.sum((running - 1.0) * onehot, axis=-1)
    slot_hot = (
        slot_pos[:, :, None] == jnp.arange(capacity, dtype=jnp.float32)[None, None, :]
    ).astype(jnp.float32)
    placer = (onehot[:, :, :, None] * slot_hot[:, :, None, :]).reshape(
        micro_count, tok_count, experts * capacity
    )
    placer = placer.astype(jnp.bfloat16)
    buffer = jnp.einsum("mtk,mtd->mkd", placer, tokens, preferred_element_type=jnp.float32)
    buffer = buffer.astype(jnp.bfloat16).reshape(micro_count, experts, capacity, model_width)
    arrived = lax.all_to_all(buffer, EXPERT, split_axis=1, concat_axis=1, tiled=True)
    token_rows = arrived.reshape(-1, model_width)
    columns = token_rows
    pre_act = jnp.dot(
        columns, lax.all_gather(w_in, DP, axis=1, tiled=True)[0], preferred_element_type=jnp.float32
    )
    hidden = jax.nn.gelu(pre_act, approximate=True).astype(jnp.bfloat16)
    columns = hidden
    served = jnp.dot(
        columns,
        lax.all_gather(w_out, DP, axis=1, tiled=True)[0],
        preferred_element_type=jnp.float32,
    )
    served = served.astype(jnp.bfloat16).reshape(arrived.shape)
    returned = lax.all_to_all(served, EXPERT, split_axis=1, concat_axis=1, tiled=True)
    returned = returned.reshape(micro_count, experts * capacity, model_width)
    combined = jnp.einsum("mtk,mkd->mtd", placer, returned, preferred_element_type=jnp.float32)
    mixed = (combined * gating[:, :, None]).astype(jnp.bfloat16)
    exps = jnp.exp(logits)
    router_probs = exps / jnp.sum(exps, axis=-1, keepdims=True)
    modal_hot = (modality[:, :, None] == jnp.arange(2, dtype=jnp.int32)[None, None, :]).astype(
        jnp.float32
    )
    counts = jnp.einsum("mtk,mte->ke", modal_hot, onehot, precision=lax.Precision.HIGHEST)
    prob_sums = jnp.einsum("mtk,mte->ke", modal_hot, router_probs, precision=lax.Precision.HIGHEST)
    modal_counts = jnp.sum(modal_hot, axis=(0, 1))
    counts, prob_sums, modal_counts = (
        over_axes(counts, EXPERT_DP),
        over_axes(prob_sums, EXPERT_DP),
        over_axes(modal_counts, EXPERT_DP),
    )
    load = jnp.stack(
        [experts * counts / modal_counts[:, None], experts * prob_sums / modal_counts[:, None]]
    )
    return (mixed, load)


def solution(mesh):
    torus = Mesh(mesh.devices.reshape(4, 4, 8, 2), ("expert_0", "expert_1", "dp_0", "dp_1"))
    in_specs = (
        P(None, EXPERT_DP, None),
        P(None, EXPERT_DP),
        P(None, EXPERT_DP, None),
        P(),
        P(EXPERT, DP, None),
        P(EXPERT, DP, None),
    )
    out_specs = (P(None, EXPERT_DP, None), P())
    return jax.shard_map(
        on_device, mesh=torus, in_specs=in_specs, out_specs=out_specs, check_vma=False
    )
```

profile of v0, /device:TPU:1, one launch (start us, length us, event | category | flops | bytes accessed | tf_op | source)
XLA Modules:
  0.0 258.7 jit_solution(4837752513307506845)
XLA Ops:
  7.2 0.0 copy-start
  7.2 0.0 all-gather.5.cloned.1.call-start
  7.2 0.7 all-gather.5.cloned.1.call-update
  7.9 0.0 all-gather.3.cloned.1.call-start
  8.0 0.7 all-gather.3.cloned.1.call-update
  8.7 0.7 fusion.30
  9.3 0.1 copy.21
  9.5 0.2 reduce_window_sum.11
  9.6 0.1 copy.22
  9.7 0.8 fusion.29
  10.5 0.5 convolution_convert_fusion
  11.0 0.1 copy.23
  11.1 26.3 %all_to_all.10 = bf16[2,16,16,1280]{3,2,0,1:T(8,128)(2,1)S(1)} all-to-all(bf16[2,16,16,1280]{3,2,0,1:T(8,128)(2,1)S(1)} %copy.23), channel_id=1, replica_groups=mesh['expert_0'=4,'expert_1'=4,'dp_0'=8,'dp_1'=2] {'expert_0','expert_1'}, dimensions={1} | all-to-all | bytes 2621440 | tf_op jit(solution)/shard_map/all_to_all | solution.py:36
  37.5 0.1 copy.24
  37.6 54.6 %all-gather.5.cloned.1.call-done = bf16[1,5120,1280]{2,1,0:T(8,128)(2,1)} async-done(((bf16[1,320,1280]{2,1,0:T(8,128)(2,1)}), bf16[1,5120,1280]{2,1,0:T(8,128)(2,1)}) %all-gather.5.cloned.1.call-update) | async-done | bytes 13107216 | tf_op jit(solution)/shard_map/all_gather | solution.py:46
  92.1 78.5 %all-gather.3.cloned.1.call-done = bf16[1,1280,5120]{2,1,0:T(8,128)(2,1)} async-done(((bf16[1,80,5120]{2,1,0:T(8,128)(2,1)}), bf16[1,1280,5120]{2,1,0:T(8,128)(2,1)}) %all-gather.3.cloned.1.call-update) | async-done | bytes 13107216 | tf_op jit(solution)/shard_map/all_gather | solution.py:40
  170.6 22.4 %fusion.20 = bf16[512,1280]{1,0:T(8,128)(2,1)S(1)} fusion(bf16[1,5120,1280]{2,1,0:T(8,128)(2,1)} %all-gather.5.cloned.1.call-done, bf16[512,1280]{1,0:T(8,128)(2,1)S(1)} %bitcast.41, bf16[1,1280,5120]{2,1,0:T(8,128)(2,1)} %all-gather.3.cloned.1.call-done), kind=kOutput, calls=%fused_computation.17 | convolution fusion | flops 13446021120 | bytes 28835840 | tf_op jit(solution)/shard_map/dot_general | solution.py:44
  193.0 0.0 copy-start.3
  193.0 1.2 copy.25
  194.2 6.5 %all-to-all-start.1 = ((bf16[2,16,16,1280]{3,2,0,1:T(8,128)(2,1)}), bf16[2,16,16,1280]{3,2,0,1:T(8,128)(2,1)S(1)}, u32[]{:S(2)}, u32[]{:S(2)}) async-start(bf16[2,16,16,1280]{3,2,0,1:T(8,128)(2,1)} %copy.25), calls=%async_computation.1 | async-start | bytes 2621440 | tf_op jit(solution)/shard_map/all_to_all | solution.py:50
  200.8 0.1 convert_reduce_fusion
  200.9 0.1 convolution_bitcast_fusion.1
  201.0 0.3 exponential_reduce_fusion
  201.4 0.1 convolution_bitcast_fusion
  201.5 18.4 %all-reduce.2 = (f32[2,16]{1,0:T(2,128)S(1)}, f32[2]{0:T(128)S(1)}, f32[2,16]{1,0:T(2,128)S(1)}) all-reduce(f32[2,16]{1,0:T(2,128)S(1)} %convolution_bitcast_fusion, f32[2]{0:T(128)S(1)} %convert_reduce_fusion, f32[2,16]{1,0:T(2,128)S(1)} %convolution_bitcast_fusion.1), channel_id=1, replica_groups=mesh['expert_0'=4,'expert_1'=4,'dp_0'=8,'dp_1'=2] {'expert_0'}, use_global_device_ids=true, to_apply=%region_13.14 | all-reduce | flops 66 | bytes 528 | tf_op jit(solution)/shard_map/psum | solution.py:14
  219.9 8.1 %all-reduce.1 = (f32[2,16]{1,0:T(2,128)S(1)}, f32[2]{0:T(128)S(1)}, f32[2,16]{1,0:T(2,128)S(1)}) all-reduce(f32[2,16]{1,0:T(2,128)S(1)} %get-tuple-element.10, f32[2]{0:T(128)S(1)} %get-tuple-element.11, f32[2,16]{1,0:T(2,128)S(1)} %get-tuple-element.12), channel_id=1, replica_groups=mesh['expert_0'=4,'expert_1'=4,'dp_0'=8,'dp_1'=2] {'expert_1'}, use_global_device_ids=true, to_apply=%region_14.15 | all-reduce | flops 66 | bytes 528 | tf_op jit(solution)/shard_map/psum | solution.py:14
  227.9 11.8 %all-reduce = (f32[2,16]{1,0:T(2,128)S(1)}, f32[2]{0:T(128)S(1)}, f32[2,16]{1,0:T(2,128)S(1)}) all-reduce(f32[2,16]{1,0:T(2,128)S(1)} %get-tuple-element.7, f32[2]{0:T(128)S(1)} %get-tuple-element.8, f32[2,16]{1,0:T(2,128)S(1)} %get-tuple-element.9), channel_id=1, replica_groups=mesh['expert_0'=4,'expert_1'=4,'dp_0'=8,'dp_1'=2] {'dp_0'}, use_global_device_ids=true, to_apply=%region_15.16 | all-reduce | flops 66 | bytes 528 | tf_op jit(solution)/shard_map/psum | solution.py:14
  239.7 10.2 %all-reduce.3 = (f32[2,16]{1,0:T(2,128)S(1)}, f32[2]{0:T(128)S(1)}, f32[2,16]{1,0:T(2,128)S(1)}) all-reduce(f32[2,16]{1,0:T(2,128)S(1)} %get-tuple-element.4, f32[2]{0:T(128)S(1)} %get-tuple-element.5, f32[2,16]{1,0:T(2,128)S(1)} %get-tuple-element.6), channel_id=1, replica_groups=mesh['expert_0'=4,'expert_1'=4,'dp_0'=8,'dp_1'=2] {'dp_1'}, use_global_device_ids=true, to_apply=%region_16.17 | all-reduce | flops 66 | bytes 528 | tf_op jit(solution)/shard_map/psum | solution.py:14
  249.9 0.1 divide_bitcast_fusion.1
  249.9 0.6 pad_maximum_fusion
  250.5 0.1 copy.26
  250.6 1.2 fusion.25
  (9 shorter events, 0.1 us)
Async XLA Ops:
  7.2 3.3 %copy-start = (bf16[2,128,1280]{2,1,0:T(8,128)(2,1)S(1)}, bf16[2,128,1280]{2,1,0:T(8,128)(2,1)}, u32[]{:S(2)}) copy-start(bf16[2,128,1280]{2,1,0:T(8,128)(2,1)} %param.6) | copy-start | bytes 1966084
  7.2 84.9 %all-gather.5.cloned.1.call-start = ((), (), s32[]{:S(2)}) async-start(), calls=%async_computation.3 | async-start | bytes 13926400 | tf_op jit(solution)/shard_map/all_gather | solution.py:46
  7.9 162.7 %all-gather.3.cloned.1.call-start = ((), (), s32[]{:S(2)}) async-start(), calls=%async_computation.2 | async-start | bytes 13926400 | tf_op jit(solution)/shard_map/all_gather | solution.py:40
  193.0 7.8 %copy-start.3 = (s32[2,128]{1,0:T(2,128)S(1)}, s32[2,128]{1,0:T(2,128)}, u32[]{:S(2)}) copy-start(s32[2,128]{1,0:T(2,128)} %param.7) | copy-start | bytes 3076
  193.0 7.9 %copy-start.2 = (s32[2,128,1]{1,2,0:T(1,128)S(1)}, s32[2,128,1]{1,2,0:T(1,128)}, u32[]{:S(2)}) copy-start(s32[2,128,1]{1,2,0:T(1,128)} %param.8) | copy-start | bytes 3076
  193.0 8.0 %copy-start.1 = (bf16[1280,16]{0,1:T(8,128)(2,1)S(1)}, bf16[1280,16]{0,1:T(8,128)(2,1)}, u32[]{:S(2)}) copy-start(bf16[1280,16]{0,1:T(8,128)(2,1)} %param.9) | copy-start | bytes 122884
  194.2 56.3 %all-to-all-start.1 = ((bf16[2,16,16,1280]{3,2,0,1:T(8,128)(2,1)}), bf16[2,16,16,1280]{3,2,0,1:T(8,128)(2,1)S(1)}, u32[]{:S(2)}, u32[]{:S(2)}) async-start(bf16[2,16,16,1280]{3,2,0,1:T(8,128)(2,1)} %copy.25), calls=%async_computation.1 | async-start | bytes 2621440 | tf_op jit(solution)/shard_map/all_to_all | solution.py:50
Sparse Core Ops, SparseCore 0:
  9.8 82.2 all-gather.4
  93.9 76.5 all-gather.2
where the time goes:
time: 259 us
  waiting for transfers between devices  134 us (52%)
  blocking collectives  74.7 us (29%)
  matrix products  24.7 us (10%)
  between operations  14.2 us (5%)
  starting transfers between devices  6.6 us (3%)
    all_gather x1, waiting for transfers between devices, on_device(): lax.all_gather(w_in, DP, axis=1, tiled=True)[0]  78.5 us
    all_gather x1, waiting for transfers between devices, on_device(): lax.all_gather(w_out, DP, axis=1, tiled=True)[0]  54.6 us
    psum x4, blocking collectives, over_axes(): shard = lax.psum(shard, axis)  48.4 us
    all_to_all x1, blocking collectives, on_device(): lax.all_to_all(buffer, EXPERT, split_axis=1, concat_axis=1, tiled=True)  26.3 us
    dot_general x1, matrix products, on_device(): jnp.dot(columns, lax.all_gather(w_out, DP, axis=1, tiled=True)[0], prefer...  22.4 us
    all_to_all x1, starting transfers between devices, on_device(): lax.all_to_all(served, EXPERT, split_axis=1, concat_axis=1, tiled=True)  6.52 us
  transfers between devices with their start and end apart: 3, of which 2 were waited for; matrix products, arithmetic and copies ran while one was open for 2% of the time, Pallas kernels for 0%

commit v1 on v0

--- a/solution.py
+++ b/solution.py
@@ -11,7 +11,7 @@
 
 def over_axes(shard, axes):
     for axis in axes:
-        shard = lax.psum(shard, axis)
+        shard = jnp.sum(lax.all_gather(shard, axis), axis=0)
     return shard
 
 

time: 259 us -> 290 us (1.12)
  blocking collectives: 74.7 us -> 131 us
  waiting for transfers between devices: 134 us -> 93.1 us
  starting transfers between devices: 6.6 us -> 14.2 us
  local copies, waits for them, and re-layouts: 1.69 us -> 6.42 us
    all_gather x0 -> x8, blocking collectives: none -> 78.1 us  [over_axes(): shard = jnp.sum(lax.all_gather(shard, axis), axis=0)]
    unnamed x0 -> x4, blocking collectives: none -> 52.9 us
    psum x4 -> x0, blocking collectives: 48.4 us -> none  [over_axes(): shard = lax.psum(shard, axis)]
    all_gather x1, waiting for transfers between devices: 54.6 us -> 13.3 us  [on_device(): lax.all_gather(w_out, DP, axis=1, tiled=True)[0]]
    all_to_all x1 -> x0, blocking collectives: 26.3 us -> none  [on_device(): lax.all_to_all(buffer, EXPERT, split_axis=1, concat_axis=1, tiled=True)]
    all_to_all x0 -> x1, starting transfers between devices: none -> 7.57 us  [on_device(): lax.all_to_all(buffer, EXPERT, split_axis=1, concat_axis=1, tiled=True)]
    unnamed x8 -> x28, local copies, waits for them, and re-layouts: 0.03 us -> 3.37 us
  transfers between devices with their start and end apart: 3 -> 4, of which waited for: 2 -> 2; matrix products, arithmetic and copies ran while one was open for 2% -> 3% of each run, Pallas kernels for 0% -> 0%
where the time goes in v1:
time: 290 us; the launch traced here: 289 us
  blocking collectives  131 us (45%)
  waiting for transfers between devices  93.1 us (32%)
  matrix products  24.9 us (9%)
  between operations  16.9 us (6%)
  starting transfers between devices  14.2 us (5%)
  local copies, waits for them, and re-layouts  6.42 us (2%)
    all_gather x1, waiting for transfers between devices, on_device(): lax.all_gather(w_in, DP, axis=1, tiled=True)[0]  78.5 us
    all_gather x8, blocking collectives, over_axes(): shard = jnp.sum(lax.all_gather(shard, axis), axis=0)  78.1 us
    unnamed x4, blocking collectives  52.9 us
    dot_general x1, matrix products, on_device(): jnp.dot(columns, lax.all_gather(w_out, DP, axis=1, tiled=True)[0], prefer...  22.6 us
    all_gather x1, waiting for transfers between devices, on_device(): lax.all_gather(w_out, DP, axis=1, tiled=True)[0]  13.3 us
    all_to_all x1, starting transfers between devices, on_device(): lax.all_to_all(buffer, EXPERT, split_axis=1, concat_axis=1, tiled=True)  7.57 us
    all_to_all x1, starting transfers between devices, on_device(): lax.all_to_all(served, EXPERT, split_axis=1, concat_axis=1, tiled=True)  6.53 us
  transfers between devices with their start and end apart: 4, of which 2 were waited for; matrix products, arithmetic and copies ran while one was open for 3% of the time, Pallas kernels for 0%

profile of v1, /device:TPU:1, one launch (start us, length us, event | category | flops | bytes accessed | tf_op | source)
XLA Modules:
  0.0 289.1 jit_solution(3611102309069886487)
XLA Ops:
  7.3 0.7 all-gather.25.cloned.1.call-update
  8.0 0.7 all-gather.23.cloned.1.call-update
  8.7 0.7 fusion.30
  9.8 0.8 fusion.29
  10.6 0.5 convolution_convert_fusion
  11.1 1.2 copy.23
  12.2 7.6 %all-to-all-start = ((bf16[2,16,16,1280]{3,2,0,1:T(8,128)(2,1)}), bf16[2,16,16,1280]{3,2,0,1:T(8,128)(2,1)S(1)}, u32[]{:S(2)}, u32[]{:S(2)}) async-start(bf16[2,16,16,1280]{3,2,0,1:T(8,128)(2,1)} %copy.23), calls=%async_computation | async-start | bytes 2621440 | tf_op jit(solution)/shard_map/all_to_all | solution.py:36
  19.8 0.6 dynamic-slice
  21.4 17.2 %all-reduce = f32[8]{0:T(128)S(1)} all-reduce(f32[8]{0:T(128)S(1)} %dynamic-update-slice), channel_id=6, replica_groups=mesh['expert_0'=4,'expert_1'=4,'dp_0'=8,'dp_1'=2] {'expert_0'}, use_global_device_ids=true, to_apply=%add | all-reduce | flops 8 | bytes 64
  38.8 0.6 dynamic-slice.1
  40.3 9.3 %all-reduce.1 = f32[8]{0:T(128)S(1)} all-reduce(f32[8]{0:T(128)S(1)} %dynamic-update-slice.1), channel_id=7, replica_groups=mesh['expert_0'=4,'expert_1'=4,'dp_0'=8,'dp_1'=2] {'expert_1'}, use_global_device_ids=true, to_apply=%add.1 | all-reduce | flops 8 | bytes 64
  49.6 0.6 dynamic-slice.2
  50.9 0.2 dynamic-update-slice.2
  51.1 18.7 %all-reduce.2 = f32[16]{0:T(128)S(1)} all-reduce(f32[16]{0:T(128)S(1)} %dynamic-update-slice.2), channel_id=8, replica_groups=mesh['expert_0'=4,'expert_1'=4,'dp_0'=8,'dp_1'=2] {'dp_0'}, use_global_device_ids=true, to_apply=%add.2 | all-reduce | flops 16 | bytes 128
  69.9 0.6 dynamic-slice.3
  71.4 7.7 %all-reduce.3 = f32[4]{0:T(128)S(1)} all-reduce(f32[4]{0:T(128)S(1)} %dynamic-update-slice.3), channel_id=9, replica_groups=mesh['expert_0'=4,'expert_1'=4,'dp_0'=8,'dp_1'=2] {'dp_1'}, use_global_device_ids=true, to_apply=%add.3 | all-reduce | flops 4 | bytes 32
  79.3 13.3 %all-gather.25.cloned.1.call-done = bf16[1,5120,1280]{2,1,0:T(8,128)(2,1)} async-done(((bf16[1,320,1280]{2,1,0:T(8,128)(2,1)}), bf16[1,5120,1280]{2,1,0:T(8,128)(2,1)}) %all-gather.25.cloned.1.call-update) | async-done | bytes 13107216 | tf_op jit(solution)/shard_map/all_gather | solution.py:46
  92.5 78.5 %all-gather.23.cloned.1.call-done = bf16[1,1280,5120]{2,1,0:T(8,128)(2,1)} async-done(((bf16[1,80,5120]{2,1,0:T(8,128)(2,1)}), bf16[1,1280,5120]{2,1,0:T(8,128)(2,1)}) %all-gather.23.cloned.1.call-update) | async-done | bytes 13107216 | tf_op jit(solution)/shard_map/all_gather | solution.py:40
  171.0 22.6 %fusion.20 = bf16[512,1280]{1,0:T(8,128)(2,1)S(1)} fusion(bf16[1,5120,1280]{2,1,0:T(8,128)(2,1)} %all-gather.25.cloned.1.call-done, bf16[512,1280]{1,0:T(8,128)(2,1)S(1)} %bitcast.53, bf16[1,1280,5120]{2,1,0:T(8,128)(2,1)} %all-gather.23.cloned.1.call-done), kind=kOutput, calls=%fused_computation.17 | convolution fusion | flops 13446021120 | bytes 28835840 | tf_op jit(solution)/shard_map/dot_general | solution.py:44
  193.6 1.2 copy.25
  194.8 6.5 %all-to-all-start.1 = ((bf16[2,16,16,1280]{3,2,0,1:T(8,128)(2,1)}), bf16[2,16,16,1280]{3,2,0,1:T(8,128)(2,1)S(1)}, u32[]{:S(2)}, u32[]{:S(2)}) async-start(bf16[2,16,16,1280]{3,2,0,1:T(8,128)(2,1)} %copy.25), calls=%async_computation.1 | async-start | bytes 2621440 | tf_op jit(solution)/shard_map/all_to_all | solution.py:50
  201.5 18.5 %all-gather.12 = f32[4,2,16]{2,1,0:T(2,128)S(1)} all-gather(f32[1,2,16]{2,1,0:T(2,128)S(1)} %convolution_bitcast_fusion.1), channel_id=2, replica_groups=mesh['expert_0'=4,'expert_1'=4,'dp_0'=8,'dp_1'=2] {'expert_0'}, dimensions={0}, use_global_device_ids=true | all-gather | bytes 640 | tf_op jit(solution)/shard_map/all_gather | solution.py:14
  220.1 7.6 %all-gather.13 = f32[4,2,16]{2,1,0:T(2,128)S(1)} all-gather(f32[1,2,16]{2,1,0:T(2,128)S(1)} %bitcast.63), channel_id=3, replica_groups=mesh['expert_0'=4,'expert_1'=4,'dp_0'=8,'dp_1'=2] {'expert_1'}, dimensions={0}, use_global_device_ids=true | all-gather | bytes 640 | tf_op jit(solution)/shard_map/all_gather | solution.py:14
  227.7 10.9 %all-gather.14 = f32[8,2,16]{2,1,0:T(2,128)S(1)} all-gather(f32[1,2,16]{2,1,0:T(2,128)S(1)} %bitcast.64), channel_id=4, replica_groups=mesh['expert_0'=4,'expert_1'=4,'dp_0'=8,'dp_1'=2] {'dp_0'}, dimensions={0}, use_global_device_ids=true | all-gather | bytes 1152 | tf_op jit(solution)/shard_map/all_gather | solution.py:14
  238.6 9.5 %all-gather.15 = f32[2,2,16]{2,1,0:T(2,128)S(1)} all-gather(f32[1,2,16]{2,1,0:T(2,128)S(1)} %bitcast.61), channel_id=5, replica_groups=mesh['expert_0'=4,'expert_1'=4,'dp_0'=8,'dp_1'=2] {'dp_1'}, dimensions={0}, use_global_device_ids=true | all-gather | bytes 384 | tf_op jit(solution)/shard_map/all_gather | solution.py:14
  248.2 0.3 exponential_reduce_fusion
  248.7 6.7 %all-gather.16 = f32[4,2,16]{2,1,0:T(2,128)S(1)} all-gather(f32[1,2,16]{2,1,0:T(2,128)S(1)} %convolution_bitcast_fusion), channel_id=10, replica_groups=mesh['expert_0'=4,'expert_1'=4,'dp_0'=8,'dp_1'=2] {'expert_0'}, dimensions={0}, use_global_device_ids=true | all-gather | bytes 640 | tf_op jit(solution)/shard_map/all_gather | solution.py:14
  255.4 5.2 %all-gather.17 = f32[4,2,16]{2,1,0:T(2,128)S(1)} all-gather(f32[1,2,16]{2,1,0:T(2,128)S(1)} %bitcast.65), channel_id=11, replica_groups=mesh['expert_0'=4,'expert_1'=4,'dp_0'=8,'dp_1'=2] {'expert_1'}, dimensions={0}, use_global_device_ids=true | all-gather | bytes 640 | tf_op jit(solution)/shard_map/all_gather | solution.py:14
  260.7 10.5 %all-gather.18 = f32[8,2,16]{2,1,0:T(2,128)S(1)} all-gather(f32[1,2,16]{2,1,0:T(2,128)S(1)} %bitcast.66), channel_id=12, replica_groups=mesh['expert_0'=4,'expert_1'=4,'dp_0'=8,'dp_1'=2] {'dp_0'}, dimensions={0}, use_global_device_ids=true | all-gather | bytes 1152 | tf_op jit(solution)/shard_map/all_gather | solution.py:14
  271.2 9.1 %all-gather.19 = f32[2,2,16]{2,1,0:T(2,128)S(1)} all-gather(f32[1,2,16]{2,1,0:T(2,128)S(1)} %bitcast.62), channel_id=13, replica_groups=mesh['expert_0'=4,'expert_1'=4,'dp_0'=8,'dp_1'=2] {'dp_1'}, dimensions={0}, use_global_device_ids=true | all-gather | bytes 384 | tf_op jit(solution)/shard_map/all_gather | solution.py:14
  280.3 0.6 pad_maximum_fusion
  281.0 1.2 fusion.25
  (54 shorter events, 2.4 us)
Async XLA Ops:
  7.2 3.4 %copy-start = (bf16[2,128,1280]{2,1,0:T(8,128)(2,1)S(1)}, bf16[2,128,1280]{2,1,0:T(8,128)(2,1)}, u32[]{:S(2)}) copy-start(bf16[2,128,1280]{2,1,0:T(8,128)(2,1)} %param.6) | copy-start | bytes 1966084
  7.2 12.7 %copy-start.7 = (u32[256]{0:T(256)S(1)}, u32[256]{0:T(256)}, u32[]{:S(2)}) copy-start(u32[256]{0:T(256)} %constant.28) | copy-start | bytes 3076
  7.2 31.6 %copy-start.6 = (u32[256]{0:T(256)S(1)}, u32[256]{0:T(256)}, u32[]{:S(2)}) copy-start(u32[256]{0:T(256)} %constant.33) | copy-start | bytes 3076
  7.2 42.4 %copy-start.5 = (u32[256]{0:T(256)S(1)}, u32[256]{0:T(256)}, u32[]{:S(2)}) copy-start(u32[256]{0:T(256)} %constant.38) | copy-start | bytes 3076
  7.2 62.7 %copy-start.4 = (u32[256]{0:T(256)S(1)}, u32[256]{0:T(256)}, u32[]{:S(2)}) copy-start(u32[256]{0:T(256)} %constant.43) | copy-start | bytes 3076
  7.2 13.9 %copy-start.3 = (s32[2,128]{1,0:T(2,128)S(1)}, s32[2,128]{1,0:T(2,128)}, u32[]{:S(2)}) copy-start(s32[2,128]{1,0:T(2,128)} %param.7) | copy-start | bytes 3076
  7.2 85.3 %all-gather.25.cloned.1.call-start = ((), (), s32[]{:S(2)}) async-start(), calls=%async_computation.3 | async-start | bytes 13926400 | tf_op jit(solution)/shard_map/all_gather | solution.py:46
  8.0 163.0 %all-gather.23.cloned.1.call-start = ((), (), s32[]{:S(2)}) async-start(), calls=%async_computation.2 | async-start | bytes 13926400 | tf_op jit(solution)/shard_map/all_gather | solution.py:40
  12.2 66.9 %all-to-all-start = ((bf16[2,16,16,1280]{3,2,0,1:T(8,128)(2,1)}), bf16[2,16,16,1280]{3,2,0,1:T(8,128)(2,1)S(1)}, u32[]{:S(2)}, u32[]{:S(2)}) async-start(bf16[2,16,16,1280]{3,2,0,1:T(8,128)(2,1)} %copy.23), calls=%async_computation | async-start | bytes 2621440 | tf_op jit(solution)/shard_map/all_to_all | solution.py:36
  193.6 7.8 %copy-start.2 = (s32[2,128,1]{1,2,0:T(1,128)S(1)}, s32[2,128,1]{1,2,0:T(1,128)}, u32[]{:S(2)}) copy-start(s32[2,128,1]{1,2,0:T(1,128)} %param.8) | copy-start | bytes 3076
  193.6 54.6 %copy-start.1 = (bf16[1280,16]{0,1:T(8,128)(2,1)S(1)}, bf16[1280,16]{0,1:T(8,128)(2,1)}, u32[]{:S(2)}) copy-start(bf16[1280,16]{0,1:T(8,128)(2,1)} %param.9) | copy-start | bytes 122884
  194.8 86.1 %all-to-all-start.1 = ((bf16[2,16,16,1280]{3,2,0,1:T(8,128)(2,1)}), bf16[2,16,16,1280]{3,2,0,1:T(8,128)(2,1)S(1)}, u32[]{:S(2)}, u32[]{:S(2)}) async-start(bf16[2,16,16,1280]{3,2,0,1:T(8,128)(2,1)} %copy.25), calls=%async_computation.1 | async-start | bytes 2621440 | tf_op jit(solution)/shard_map/all_to_all | solution.py:50
Sparse Core Ops, SparseCore 0:
  9.9 82.5 all-gather.24
  94.4 76.5 all-gather.22
